TPU v7x, 32 devices: a whole 2x2x4 slice. The times are simulated.
32 devices in a mesh: wide: 8 (over y, x, core), narrow: 4 (over z).
Axes of the slice: x: 2, y: 2, z: 4, core: 2. Of those that a mesh axis runs over, the one named last changes fastest.
Arguments:
- image: bfloat16 [2, 256, 256, 256], P(None, 'wide', 'narrow'), may hold values from -6 to 6
- deapodization: float32 [3, 256], replicated, may hold values from 0.5 to 2
- offsets: int32 [32, 8], P(('wide', 'narrow')), may hold values from 0 to 256
- cross_weight: bfloat16 [32, 8, 1536, 1024], P(('wide', 'narrow')), may hold values from -0.1875 to 0.1875
- x_weight: bfloat16 [32, 8, 1536, 256], P(('wide', 'narrow')), may hold values from -0.375 to 0.375
Outputs:
- samples: float32 [32, 8, 2, 1536], P(('wide', 'narrow'))
Inputs may be any that keep to these rules, and one draw needn't show every extreme that they name: `offsets`: each entry is the first row, along the first frequency dimension, of a group's window of 256 rows in one slab.
All inputs are finite; a program needn't handle non-finite values.
Results may differ from a plain program's by a relative error of at most 0.007.
Values may be sent and summed in bfloat16 or wider, within the bound.
A program may use at most 128 MiB of HBM per device.

v0:
```python
import math

import jax
import jax.numpy as jnp
from jax import lax
from jax.sharding import PartitionSpec as P

G = 512
KZ = 64
BX = 256
SAMP = 1536


def shifted(block, axis, distance):
    devices = range(lax.axis_size(axis))
    route = [((i - distance) % len(devices), i) for i in devices]
    return lax.ppermute(block, axis, route)


def block_table(out_rows, inputs, grid_size, lowest):
    frequency = jnp.arange(out_rows, dtype=jnp.int32) + lowest
    position = jnp.arange(inputs, dtype=jnp.int32) - inputs // 2
    phases = jnp.mod(frequency[:, None] * position[None, :], grid_size)
    angles = phases.astype(jnp.float32) * (2.0 * math.pi / grid_size)
    factor = 1.0 / math.sqrt(inputs)
    cosine = (jnp.cos(angles) * factor).astype(jnp.bfloat16)
    sine = (jnp.sin(angles) * factor).astype(jnp.bfloat16)
    real_rows = jnp.stack([cosine, sine], axis=1)
    imag_rows = jnp.stack([-sine, cosine], axis=1)
    return jnp.stack([real_rows, imag_rows], axis=0)


def window_samples(window_rows, cross_rows, window_gain):
    partial_value = jnp.einsum(
        "ms,qcs->cmq", cross_rows, window_rows, preferred_element_type=jnp.float32
    )
    return jnp.sum(partial_value * window_gain.astype(jnp.float32)[None], axis=-1)


def per_device(image, deapodization, offsets, cross_weight, x_weight):
    wide_count = lax.axis_size("wide")
    wide_index = lax.axis_index("wide")
    narrow_index = lax.axis_index("narrow")
    block_x = image.shape[1]
    block_y = image.shape[2]
    image_width = image.shape[3]
    scale_x = lax.dynamic_slice_in_dim(deapodization[0], wide_index * block_x, block_x)
    scale_y = lax.dynamic_slice_in_dim(deapodization[1], narrow_index * block_y, block_y)
    weighted = (
        image.astype(jnp.float32)
        * scale_x[None, :, None, None]
        * scale_y[None, None, :, None]
        * deapodization[2][None, None, None, :]
    ).astype(jnp.bfloat16)
    z_table = block_table(KZ, image_width, G, -(KZ // 2))
    band_data = (
        jnp.einsum("okcz,cxyz->xyko", z_table, weighted, preferred_element_type=jnp.float32)
        .astype(jnp.bfloat16)
        .reshape(block_x, block_y, 2 * KZ)
    )
    line_table = block_table(G, image_width, G, -(G // 2))
    pieces = lax.all_to_all(band_data, "narrow", split_axis=2, concat_axis=1, tiled=True)
    item_count = pieces.shape[0]
    band_depth = pieces.shape[2] // 2
    unpacked = pieces.reshape(item_count, image_width, band_depth, 2)
    product = jnp.einsum(
        "oqcy,xykc->xoqk", line_table, unpacked, preferred_element_type=jnp.float32
    )
    columns = product.astype(jnp.bfloat16).reshape(item_count, 2, G * band_depth)
    slab_lines = lax.all_to_all(columns, "wide", split_axis=2, concat_axis=0, tiled=True)

    def transform_rows(table_rows, source):
        product = jnp.einsum(
            "opcx,xcs->pos", table_rows, source, preferred_element_type=jnp.float32
        )
        return product.astype(jnp.bfloat16)

    def slab_samples(slab_data, slab_index):
        start_row = lax.dynamic_index_in_dim(offsets[0], slab_index, 0, False)
        cross_rows = lax.dynamic_index_in_dim(cross_weight[0], slab_index, 0, False)
        window_gain = lax.dynamic_index_in_dim(x_weight[0], slab_index, 0, False)
        part_table = block_table(BX, image_width, G, start_row - G // 2)
        window_rows = transform_rows(part_table, slab_data)
        return window_samples(window_rows, cross_rows, window_gain)

    def record(results, slab_data, slab_index):
        return lax.dynamic_update_index_in_dim(
            results, slab_samples(slab_data, slab_index), slab_index, 0
        )

    results = jnp.zeros((wide_count, 2, SAMP), jnp.float32)

    def one_hop(hop_count, carried):
        current, results = carried
        incoming = shifted(current, "wide", 1)
        results = record(results, current, jnp.mod(wide_index - hop_count, wide_count))
        return (incoming, results)

    current, results = lax.fori_loop(0, wide_count - 1, one_hop, (slab_lines, results))
    results = record(results, current, jnp.mod(wide_index - (wide_count - 1), wide_count))
    return results[None]


def solution(mesh):
    return jax.shard_map(
        per_device,
        mesh=mesh,
        in_specs=(
            P(None, "wide", "narrow", None),
            P(),
            P(("wide", "narrow"), None),
            P(("wide", "narrow"), None, None, None),
            P(("wide", "narrow"), None, None, None),
        ),
        out_specs=P(("wide", "narrow"), None, None, None),
        check_vma=False,
    )
```

profile of v0, /device:TPU:0, one launch (start us, length us, event | category | flops | bytes accessed | tf_op | source)
XLA Modules:
  0.0 221.7 jit_solution(11140627748605231871)
XLA Ops:
  3.5 2.5 %fusion.34 = bf16[32,64,64,2]{2,1,3,0:T(8,128)(2,1)S(1)} fusion(bf16[1,64,2,256]{3,1,2,0:T(8,128)(2,1)S(1)} %get-tuple-element.269, bf16[1,64,2,256]{3,1,2,0:T(8,128)(2,1)S(1)} %get-tuple-element.268, bf16[2,32,64,256]{3,2,1,0:T(8,128)(2,1)} %param.7, f32[256]{0:T(256)S(1)} %bitcast.160, f32[64]{0:T(128)S(1)} %fusion.67, f32[32]{0:T(128)S(1)} %fusion.66), kind=kOutput, calls=%fused_computation.44 | convolution fusion | flops 274202624 | bytes 2753920 | tf_op jit(solution)/shard_map/okcz,cxyz->xyko/dot_general | solution.py:57
  6.1 1.6 copy.31
  7.7 1.5 reshape.794
  9.3 6.3 %all-to-all-start = ((bf16[4,2,32768]{2,1,0:T(2,128)(2,1)}), bf16[4,2,32768]{2,1,0:T(2,128)(2,1)S(1)}, u32[]{:S(2)}, u32[]{:S(2)}) async-start(bf16[4,2,32768]{2,1,0:T(2,128)(2,1)} %reshape.794), calls=%async_computation | async-start | bytes 1048576 | tf_op jit(solution)/shard_map/all_to_all | solution.py:62
  15.6 2.2 fusion.62
  17.8 2.5 %multiply_convert_fusion.3 = (bf16[512,1,256]{2,0,1:T(8,128)(2,1)S(1)}, bf16[512,1,256]{2,0,1:T(8,128)(2,1)S(1)}) fusion(s32[256]{0:T(256)S(1)} %get-tuple-element.280, s32[512]{0:T(512)S(1)} %iota_add_fusion.2), kind=kLoop, calls=%fused_computation.66 | loop fusion | flops 2359296 | bytes 527360 | tf_op jit(solution)/shard_map/convert_element_type | solution.py:27
  20.5 9.6 %all-to-all-done = bf16[4,2,32768]{2,1,0:T(2,128)(2,1)S(1)} async-done(((bf16[4,2,32768]{2,1,0:T(2,128)(2,1)}), bf16[4,2,32768]{2,1,0:T(2,128)(2,1)S(1)}, u32[]{:S(2)}, u32[]{:S(2)}) %all-to-all-start) | async-done | bytes 524320 | tf_op jit(solution)/shard_map/all_to_all | solution.py:62
  31.7 1.5 reshape.778
  33.1 1.8 fusion.37
  35.0 5.1 %copy.35 = bf16[32,2,512,16]{0,3,2,1:T(8,128)(2,1)} copy(bf16[32,2,512,16]{2,3,1,0:T(8,128)(2,1)S(1)} %fusion.37) | data formatting | bytes 2097152 | tf_op jit(solution)/shard_map/convert_element_type | solution.py:69
  40.0 10.1 %copy.69 = bf16[32,2,8192]{0,1,2:T(2,128)(2,1)} copy(bf16[32,2,8192]{0,2,1:T(8,128)(2,1)} %bitcast.154) | data formatting | bytes 2097152 | tf_op jit(solution)/shard_map/reshape | solution.py:69
  50.1 7.8 %reshape.796 = bf16[8,2,32768]{2,1,0:T(2,128)(2,1)} reshape(bf16[8192,2,32]{2,1,0:T(2,128)(2,1)} %bitcast.155) | data formatting | bytes 2097152
  57.9 3.7 %all-to-all-start.1 = ((bf16[8,2,32768]{2,1,0:T(2,128)(2,1)}), bf16[8,2,32768]{2,1,0:T(2,128)(2,1)S(1)}, u32[]{:S(2)}, u32[]{:S(2)}) async-start(bf16[8,2,32768]{2,1,0:T(2,128)(2,1)} %reshape.796), calls=%async_computation.1 | async-start | bytes 2097152 | tf_op jit(solution)/shard_map/all_to_all | solution.py:70
  62.9 1.7 copy.42
  65.7 1.3 multiply_convert_fusion.5
  67.0 10.0 %all-to-all-done.1 = bf16[8,2,32768]{2,1,0:T(2,128)(2,1)S(1)} async-done(((bf16[8,2,32768]{2,1,0:T(2,128)(2,1)}), bf16[8,2,32768]{2,1,0:T(2,128)(2,1)S(1)}, u32[]{:S(2)}, u32[]{:S(2)}) %all-to-all-start.1) | async-done | bytes 1048608 | tf_op jit(solution)/shard_map/all_to_all | solution.py:70
  77.0 4.5 %reshape.797 = bf16[8192,2,32]{2,1,0:T(2,128)(2,1)} reshape(bf16[8,2,32768]{2,1,0:T(2,128)(2,1)S(1)} %all-to-all-done.1) | data formatting | bytes 2097152
  81.6 10.4 %copy.57 = bf16[32,2,8,1024]{3,0,2,1:T(8,128)(2,1)} copy(bf16[32,2,8,1024]{0,1,3,2:T(2,128)(2,1)} %bitcast.153) | data formatting | bytes 2097152 | tf_op jit(solution)/shard_map/all_to_all | solution.py:70
  92.0 123.9 %while.18 = (s32[]{:T(128)}, bf16[256,2,1024]{2,0,1:T(8,128)(2,1)}, f32[8,2,1536]{2,1,0:T(2,128)S(1)}, s32[]{:T(128)}, s32[1,8]{1,0:T(1,128)S(1)}, /*index=5*/bf...) while((s32[]{:T(128)}, bf16[256,2,1024]{2,0,1:T(8,128)(2,1)}, ...), condition=%wide.region_2.3_spmd, body=%wide.region_0.2_spmd.sunk | while | flops 2152920576 | bytes 19441996 | solution.py:99
  92.0 2.3 %copy.77 = bf16[256,2,1024]{2,0,1:T(8,128)(2,1)} copy(bf16[256,2,1024]{2,0,1:T(8,128)(2,1)} %get-tuple-element.348) | data formatting | bytes 2097152 | tf_op jit(solution)/shard_map
  95.5 1.3 multiply_convert_fusion.10
  99.6 4.6 %fusion.88 = f32[2,1536]{1,0:T(2,128)S(1)} fusion(f32[1536,256]{0,1:T(8,128)S(1)} %bitcast_convert_fusion.7, bf16[1,8,1536,1024]{3,2,1,0:T(8,128)(2,1)} %get-tuple-element.363, s32[]{:T(128)S(6)} %select_n.233, bf16[256,2,1024]{2,0,1:T(8,128)(2,1)} %copy.77, bf16[1,256,2,256]{3,1,2,0:T(8,128)(2,1)S(1)} %get-tuple-element.334, ...), kind=kOutput, calls=%fused_computation.5.clone.1 | convolution fusion | flops 2149839872 | bytes 6303748 | tf_op jit(solution)/shard_map/while/body/eval_jaxpr/ms,qcs->cmq/dot_general | solution.py:34
  104.2 5.5 %collective-permute-done = bf16[256,2,1024]{2,0,1:T(8,128)(2,1)} collective-permute-done((bf16[256,2,1024]{2,0,1:T(8,128)(2,1)}, bf16[256,2,1024]{2,0,1:T(8,128)(2,1)}, u32[]{:S(2)}, u32[]{:S(2)}) %collective-permute-start) | collective-permute-done | bytes 1048608 | tf_op jit(solution)/shard_map/while/body/eval_jaxpr/ppermute | solution.py:17
  109.7 2.3 %copy.77 = bf16[256,2,1024]{2,0,1:T(8,128)(2,1)} copy(bf16[256,2,1024]{2,0,1:T(8,128)(2,1)} %get-tuple-element.348) | data formatting | bytes 2097152 | tf_op jit(solution)/shard_map
  113.2 1.3 multiply_convert_fusion.10
  117.3 4.6 %fusion.88 = f32[2,1536]{1,0:T(2,128)S(1)} fusion(f32[1536,256]{0,1:T(8,128)S(1)} %bitcast_convert_fusion.7, bf16[1,8,1536,1024]{3,2,1,0:T(8,128)(2,1)} %get-tuple-element.363, s32[]{:T(128)S(6)} %select_n.233, bf16[256,2,1024]{2,0,1:T(8,128)(2,1)} %copy.77, bf16[1,256,2,256]{3,1,2,0:T(8,128)(2,1)S(1)} %get-tuple-element.334, ...), kind=kOutput, calls=%fused_computation.5.clone.1 | convolution fusion | flops 2149839872 | bytes 6303748 | tf_op jit(solution)/shard_map/while/body/eval_jaxpr/ms,qcs->cmq/dot_general | solution.py:34
  121.9 5.5 %collective-permute-done = bf16[256,2,1024]{2,0,1:T(8,128)(2,1)} collective-permute-done((bf16[256,2,1024]{2,0,1:T(8,128)(2,1)}, bf16[256,2,1024]{2,0,1:T(8,128)(2,1)}, u32[]{:S(2)}, u32[]{:S(2)}) %collective-permute-start) | collective-permute-done | bytes 1048608 | tf_op jit(solution)/shard_map/while/body/eval_jaxpr/ppermute | solution.py:17
  127.4 2.3 %copy.77 = bf16[256,2,1024]{2,0,1:T(8,128)(2,1)} copy(bf16[256,2,1024]{2,0,1:T(8,128)(2,1)} %get-tuple-element.348) | data formatting | bytes 2097152 | tf_op jit(solution)/shard_map
  130.9 1.3 multiply_convert_fusion.10
  135.0 4.6 %fusion.88 = f32[2,1536]{1,0:T(2,128)S(1)} fusion(f32[1536,256]{0,1:T(8,128)S(1)} %bitcast_convert_fusion.7, bf16[1,8,1536,1024]{3,2,1,0:T(8,128)(2,1)} %get-tuple-element.363, s32[]{:T(128)S(6)} %select_n.233, bf16[256,2,1024]{2,0,1:T(8,128)(2,1)} %copy.77, bf16[1,256,2,256]{3,1,2,0:T(8,128)(2,1)S(1)} %get-tuple-element.334, ...), kind=kOutput, calls=%fused_computation.5.clone.1 | convolution fusion | flops 2149839872 | bytes 6303748 | tf_op jit(solution)/shard_map/while/body/eval_jaxpr/ms,qcs->cmq/dot_general | solution.py:34
  139.6 5.5 %collective-permute-done = bf16[256,2,1024]{2,0,1:T(8,128)(2,1)} collective-permute-done((bf16[256,2,1024]{2,0,1:T(8,128)(2,1)}, bf16[256,2,1024]{2,0,1:T(8,128)(2,1)}, u32[]{:S(2)}, u32[]{:S(2)}) %collective-permute-start) | collective-permute-done | bytes 1048608 | tf_op jit(solution)/shard_map/while/body/eval_jaxpr/ppermute | solution.py:17
  145.1 2.3 %copy.77 = bf16[256,2,1024]{2,0,1:T(8,128)(2,1)} copy(bf16[256,2,1024]{2,0,1:T(8,128)(2,1)} %get-tuple-element.348) | data formatting | bytes 2097152 | tf_op jit(solution)/shard_map
  148.6 1.3 multiply_convert_fusion.10
  152.7 4.6 %fusion.88 = f32[2,1536]{1,0:T(2,128)S(1)} fusion(f32[1536,256]{0,1:T(8,128)S(1)} %bitcast_convert_fusion.7, bf16[1,8,1536,1024]{3,2,1,0:T(8,128)(2,1)} %get-tuple-element.363, s32[]{:T(128)S(6)} %select_n.233, bf16[256,2,1024]{2,0,1:T(8,128)(2,1)} %copy.77, bf16[1,256,2,256]{3,1,2,0:T(8,128)(2,1)S(1)} %get-tuple-element.334, ...), kind=kOutput, calls=%fused_computation.5.clone.1 | convolution fusion | flops 2149839872 | bytes 6303748 | tf_op jit(solution)/shard_map/while/body/eval_jaxpr/ms,qcs->cmq/dot_general | solution.py:34
  157.3 5.5 %collective-permute-done = bf16[256,2,1024]{2,0,1:T(8,128)(2,1)} collective-permute-done((bf16[256,2,1024]{2,0,1:T(8,128)(2,1)}, bf16[256,2,1024]{2,0,1:T(8,128)(2,1)}, u32[]{:S(2)}, u32[]{:S(2)}) %collective-permute-start) | collective-permute-done | bytes 1048608 | tf_op jit(solution)/shard_map/while/body/eval_jaxpr/ppermute | solution.py:17
  162.8 2.3 %copy.77 = bf16[256,2,1024]{2,0,1:T(8,128)(2,1)} copy(bf16[256,2,1024]{2,0,1:T(8,128)(2,1)} %get-tuple-element.348) | data formatting | bytes 2097152 | tf_op jit(solution)/shard_map
  166.4 1.3 multiply_convert_fusion.10
  170.4 4.6 %fusion.88 = f32[2,1536]{1,0:T(2,128)S(1)} fusion(f32[1536,256]{0,1:T(8,128)S(1)} %bitcast_convert_fusion.7, bf16[1,8,1536,1024]{3,2,1,0:T(8,128)(2,1)} %get-tuple-element.363, s32[]{:T(128)S(6)} %select_n.233, bf16[256,2,1024]{2,0,1:T(8,128)(2,1)} %copy.77, bf16[1,256,2,256]{3,1,2,0:T(8,128)(2,1)S(1)} %get-tuple-element.334, ...), kind=kOutput, calls=%fused_computation.5.clone.1 | convolution fusion | flops 2149839872 | bytes 6303748 | tf_op jit(solution)/shard_map/while/body/eval_jaxpr/ms,qcs->cmq/dot_general | solution.py:34
  175.0 5.5 %collective-permute-done = bf16[256,2,1024]{2,0,1:T(8,128)(2,1)} collective-permute-done((bf16[256,2,1024]{2,0,1:T(8,128)(2,1)}, bf16[256,2,1024]{2,0,1:T(8,128)(2,1)}, u32[]{:S(2)}, u32[]{:S(2)}) %collective-permute-start) | collective-permute-done | bytes 1048608 | tf_op jit(solution)/shard_map/while/body/eval_jaxpr/ppermute | solution.py:17
  180.5 2.3 %copy.77 = bf16[256,2,1024]{2,0,1:T(8,128)(2,1)} copy(bf16[256,2,1024]{2,0,1:T(8,128)(2,1)} %get-tuple-element.348) | data formatting | bytes 2097152 | tf_op jit(solution)/shard_map
  184.1 1.3 multiply_convert_fusion.10
  188.1 4.6 %fusion.88 = f32[2,1536]{1,0:T(2,128)S(1)} fusion(f32[1536,256]{0,1:T(8,128)S(1)} %bitcast_convert_fusion.7, bf16[1,8,1536,1024]{3,2,1,0:T(8,128)(2,1)} %get-tuple-element.363, s32[]{:T(128)S(6)} %select_n.233, bf16[256,2,1024]{2,0,1:T(8,128)(2,1)} %copy.77, bf16[1,256,2,256]{3,1,2,0:T(8,128)(2,1)S(1)} %get-tuple-element.334, ...), kind=kOutput, calls=%fused_computation.5.clone.1 | convolution fusion | flops 2149839872 | bytes 6303748 | tf_op jit(solution)/shard_map/while/body/eval_jaxpr/ms,qcs->cmq/dot_general | solution.py:34
  192.7 5.5 %collective-permute-done = bf16[256,2,1024]{2,0,1:T(8,128)(2,1)} collective-permute-done((bf16[256,2,1024]{2,0,1:T(8,128)(2,1)}, bf16[256,2,1024]{2,0,1:T(8,128)(2,1)}, u32[]{:S(2)}, u32[]{:S(2)}) %collective-permute-start) | collective-permute-done | bytes 1048608 | tf_op jit(solution)/shard_map/while/body/eval_jaxpr/ppermute | solution.py:17
  198.2 2.3 %copy.77 = bf16[256,2,1024]{2,0,1:T(8,128)(2,1)} copy(bf16[256,2,1024]{2,0,1:T(8,128)(2,1)} %get-tuple-element.348) | data formatting | bytes 2097152 | tf_op jit(solution)/shard_map
  201.8 1.3 multiply_convert_fusion.10
  205.8 4.6 %fusion.88 = f32[2,1536]{1,0:T(2,128)S(1)} fusion(f32[1536,256]{0,1:T(8,128)S(1)} %bitcast_convert_fusion.7, bf16[1,8,1536,1024]{3,2,1,0:T(8,128)(2,1)} %get-tuple-element.363, s32[]{:T(128)S(6)} %select_n.233, bf16[256,2,1024]{2,0,1:T(8,128)(2,1)} %copy.77, bf16[1,256,2,256]{3,1,2,0:T(8,128)(2,1)S(1)} %get-tuple-element.334, ...), kind=kOutput, calls=%fused_computation.5.clone.1 | convolution fusion | flops 2149839872 | bytes 6303748 | tf_op jit(solution)/shard_map/while/body/eval_jaxpr/ms,qcs->cmq/dot_general | solution.py:34
  210.4 5.5 %collective-permute-done = bf16[256,2,1024]{2,0,1:T(8,128)(2,1)} collective-permute-done((bf16[256,2,1024]{2,0,1:T(8,128)(2,1)}, bf16[256,2,1024]{2,0,1:T(8,128)(2,1)}, u32[]{:S(2)}, u32[]{:S(2)}) %collective-permute-start) | collective-permute-done | bytes 1048608 | tf_op jit(solution)/shard_map/while/body/eval_jaxpr/ppermute | solution.py:17
  215.9 5.1 %fusion.29 = f32[2,1536]{1,0:T(2,128)S(1)} fusion(f32[1536,256]{0,1:T(8,128)} %copy.42, bf16[1,8,1536,1024]{3,2,1,0:T(8,128)(2,1)} %get-tuple-element.371, s32[]{:T(128)S(6)} %select_n.180, bf16[256,2,1024]{2,0,1:T(8,128)(2,1)} %get-tuple-element.215, bf16[1,256,2,256]{3,1,2,0:T(8,128)(2,1)S(1)} %get-tuple-element.267, ...), kind=kOutput, calls=%fused_computation.43 | convolution fusion | flops 2150626304 | bytes 6303748 | tf_op jit(solution)/shard_map/ms,qcs->cmq/dot_general | solution.py:34
  (85 shorter events, 36.3 us)
Async XLA Ops:
  9.3 20.8 %all-to-all-start = ((bf16[4,2,32768]{2,1,0:T(2,128)(2,1)}), bf16[4,2,32768]{2,1,0:T(2,128)(2,1)S(1)}, u32[]{:S(2)}, u32[]{:S(2)}) async-start(bf16[4,2,32768]{2,1,0:T(2,128)(2,1)} %reshape.794), calls=%async_computation | async-start | bytes 1048576 | tf_op jit(solution)/shard_map/all_to_all | solution.py:62
  57.9 19.1 %all-to-all-start.1 = ((bf16[8,2,32768]{2,1,0:T(2,128)(2,1)}), bf16[8,2,32768]{2,1,0:T(2,128)(2,1)S(1)}, u32[]{:S(2)}, u32[]{:S(2)}) async-start(bf16[8,2,32768]{2,1,0:T(2,128)(2,1)} %reshape.796), calls=%async_computation.1 | async-start | bytes 2097152 | tf_op jit(solution)/shard_map/all_to_all | solution.py:70
  81.5 10.4 %copy-start.1 = (s32[1,8]{1,0:T(1,128)S(1)}, s32[1,8]{1,0:T(1,128)}, u32[]{:S(2)}) copy-start(s32[1,8]{1,0:T(1,128)} %param.9) | copy-start | bytes 100
  94.3 15.4 %collective-permute-start = (bf16[256,2,1024]{2,0,1:T(8,128)(2,1)}, bf16[256,2,1024]{2,0,1:T(8,128)(2,1)}, u32[]{:S(2)}, u32[]{:S(2)}) collective-permute-start(bf16[256,2,1024]{2,0,1:T(8,128)(2,1)} %copy.77), channel_id=1, source_target_pairs={{28,0},{0,4},{4,8},{8,12},{12,16},{16,20},{20,24},{24,28},{29,1},{... | collective-permute-start | bytes 3145736 | tf_op jit(solution)/shard_map/while/body/eval_jaxpr/ppermute | solution.py:17
  112.0 15.4 %collective-permute-start = (bf16[256,2,1024]{2,0,1:T(8,128)(2,1)}, bf16[256,2,1024]{2,0,1:T(8,128)(2,1)}, u32[]{:S(2)}, u32[]{:S(2)}) collective-permute-start(bf16[256,2,1024]{2,0,1:T(8,128)(2,1)} %copy.77), channel_id=1, source_target_pairs={{28,0},{0,4},{4,8},{8,12},{12,16},{16,20},{20,24},{24,28},{29,1},{... | collective-permute-start | bytes 3145736 | tf_op jit(solution)/shard_map/while/body/eval_jaxpr/ppermute | solution.py:17
  129.7 15.4 %collective-permute-start = (bf16[256,2,1024]{2,0,1:T(8,128)(2,1)}, bf16[256,2,1024]{2,0,1:T(8,128)(2,1)}, u32[]{:S(2)}, u32[]{:S(2)}) collective-permute-start(bf16[256,2,1024]{2,0,1:T(8,128)(2,1)} %copy.77), channel_id=1, source_target_pairs={{28,0},{0,4},{4,8},{8,12},{12,16},{16,20},{20,24},{24,28},{29,1},{... | collective-permute-start | bytes 3145736 | tf_op jit(solution)/shard_map/while/body/eval_jaxpr/ppermute | solution.py:17
  147.4 15.4 %collective-permute-start = (bf16[256,2,1024]{2,0,1:T(8,128)(2,1)}, bf16[256,2,1024]{2,0,1:T(8,128)(2,1)}, u32[]{:S(2)}, u32[]{:S(2)}) collective-permute-start(bf16[256,2,1024]{2,0,1:T(8,128)(2,1)} %copy.77), channel_id=1, source_target_pairs={{28,0},{0,4},{4,8},{8,12},{12,16},{16,20},{20,24},{24,28},{29,1},{... | collective-permute-start | bytes 3145736 | tf_op jit(solution)/shard_map/while/body/eval_jaxpr/ppermute | solution.py:17
  165.1 15.4 %collective-permute-start = (bf16[256,2,1024]{2,0,1:T(8,128)(2,1)}, bf16[256,2,1024]{2,0,1:T(8,128)(2,1)}, u32[]{:S(2)}, u32[]{:S(2)}) collective-permute-start(bf16[256,2,1024]{2,0,1:T(8,128)(2,1)} %copy.77), channel_id=1, source_target_pairs={{28,0},{0,4},{4,8},{8,12},{12,16},{16,20},{20,24},{24,28},{29,1},{... | collective-permute-start | bytes 3145736 | tf_op jit(solution)/shard_map/while/body/eval_jaxpr/ppermute | solution.py:17
  182.8 15.4 %collective-permute-start = (bf16[256,2,1024]{2,0,1:T(8,128)(2,1)}, bf16[256,2,1024]{2,0,1:T(8,128)(2,1)}, u32[]{:S(2)}, u32[]{:S(2)}) collective-permute-start(bf16[256,2,1024]{2,0,1:T(8,128)(2,1)} %copy.77), channel_id=1, source_target_pairs={{28,0},{0,4},{4,8},{8,12},{12,16},{16,20},{20,24},{24,28},{29,1},{... | collective-permute-start | bytes 3145736 | tf_op jit(solution)/shard_map/while/body/eval_jaxpr/ppermute | solution.py:17
  200.5 15.4 %collective-permute-start = (bf16[256,2,1024]{2,0,1:T(8,128)(2,1)}, bf16[256,2,1024]{2,0,1:T(8,128)(2,1)}, u32[]{:S(2)}, u32[]{:S(2)}) collective-permute-start(bf16[256,2,1024]{2,0,1:T(8,128)(2,1)} %copy.77), channel_id=1, source_target_pairs={{28,0},{0,4},{4,8},{8,12},{12,16},{16,20},{20,24},{24,28},{29,1},{... | collective-permute-start | bytes 3145736 | tf_op jit(solution)/shard_map/while/body/eval_jaxpr/ppermute | solution.py:17
  215.9 5.1 %copy-start = (f32[8,2,1536]{2,1,0:T(2,128)}, f32[8,2,1536]{2,1,0:T(2,128)S(1)}, u32[]{:S(2)}) copy-start(f32[8,2,1536]{2,1,0:T(2,128)S(1)} %get-tuple-element.214) | copy-start | bytes 294916
where the time goes:
time: 223 us; the launch traced here: 222 us
  local copies, waits for them, and re-layouts  73.5 us (33%)
  waiting for transfers between devices  58.2 us (26%)
  matrix products  41.5 us (19%)
  other arithmetic  37.8 us (17%)
  starting transfers between devices  10.1 us (5%)
    ppermute x7, waiting for transfers between devices, shifted(): return lax.ppermute(block, axis, route)  38.5 us
    dot_general x8, matrix products, window_samples(): jnp.einsum('ms,qcs->cmq', cross_rows, window_rows, preferred_element_type...  37.1 us
    another operation x7, local copies, waits for them, and re-layouts  15.8 us
    unnamed x8, local copies, waits for them, and re-layouts  14.6 us
    convert_element_type x10, other arithmetic, block_table(): sine = (jnp.sin(angles) * factor).astype(jnp.bfloat16)  13.1 us
    neg x10, other arithmetic, block_table(): imag_rows = jnp.stack([-sine, cosine], axis=1)  11.1 us
    all_to_all x1, local copies, waits for them, and re-layouts, per_device(): lax.all_to_all(columns, 'wide', split_axis=2, concat_axis=0, tiled=True)  10.4 us
    dynamic_slice x14, local copies, waits for them, and re-layouts, slab_samples(): window_gain = lax.dynamic_index_in_dim(x_weight[0], slab_index, 0, False)  10.3 us
  transfers between devices with their start and end apart: 9, of which 9 were waited for; matrix products, arithmetic and copies ran while one was open for 36% of the time, Pallas kernels for 0%

commit v1 on v0

v1 whole, which is shorter than its diff:
```python
import functools
import math

import jax
import jax.numpy as jnp
import numpy as np
from jax import lax
from jax.experimental import pallas as pl
from jax.experimental.pallas import tpu as pltpu
from jax.sharding import PartitionSpec as P

G = 512
KZ = 64
BX = 256


def base_tables(out_rows, inputs, grid_size, lowest):
    frequency = np.arange(out_rows, dtype=np.int64) + lowest
    position = np.arange(inputs, dtype=np.int64) - inputs // 2
    phases = np.mod(frequency[:, None] * position[None, :], grid_size)
    angles = phases.astype(np.float64) * (2.0 * math.pi / grid_size)
    factor = 1.0 / math.sqrt(inputs)
    cosine = (np.cos(angles) * factor).astype(np.float32).astype(jnp.bfloat16)
    sine = (np.sin(angles) * factor).astype(np.float32).astype(jnp.bfloat16)
    return cosine, sine


def complex_table(cosine, sine):
    real_rows = np.stack([cosine, sine], axis=1)
    imag_rows = np.stack([-sine, cosine], axis=1)
    return np.stack([real_rows, imag_rows], axis=0)


def sample_kernel(
    sizes, offsets_ref, band_ref, line_ref, row_ref, x_ref, cross_ref, out_ref, wide_ref, slab_ref, window_ref
):
    depth, grid_rows, width, tile = sizes
    step = pl.program_id(0)
    cells = slab_ref.shape[0]

    @pl.when(step == 0)
    def _():
        def one_plane(k, carry):
            parts = [
                band_ref[:, piece, k].reshape(width, band_ref.shape[-1])
                for piece in range(band_ref.shape[1])
            ]
            plane = jnp.concatenate(parts, axis=-1) if len(parts) > 1 else parts[0]
            lines = lax.dot_general(
                line_ref[...], plane, (((1,), (1,)), ((), ())), preferred_element_type=jnp.float32
            )
            for part in range(2):
                for lane in range(0, width, 128):
                    wide_ref[(part * width + lane) // 128, pl.ds(k, grid_rows, stride=depth), :] = lines[
                        part * grid_rows : (part + 1) * grid_rows, lane : lane + 128
                    ]
            return carry

        for k in range(depth):
            one_plane(k, 0)

    here = pl.ds(pl.multiple_of(step * cells, cells), cells)
    start = offsets_ref[0, step]
    for block in range(2 * width // 128):
        lanes = slice(block * 128, (block + 1) * 128)
        slab_ref[:, lanes] = wide_ref[block, here, :].astype(jnp.bfloat16)
        window_ref[:, lanes] = row_ref[block, pl.ds(start, BX), :].astype(jnp.bfloat16)
    for first in range(0, cross_ref.shape[1], tile):
        rows = slice(first, first + tile)
        partial = jnp.dot(cross_ref[0, rows], slab_ref[...], preferred_element_type=jnp.float32)
        gain = jnp.dot(x_ref[0, rows], window_ref[...], preferred_element_type=jnp.float32)
        part_re, part_im = partial[:, :width], partial[:, width:]
        gain_cos, gain_sin = gain[:, :width], gain[:, width:]
        for part, value in enumerate(
            (gain_cos * part_re + gain_sin * part_im, gain_cos * part_im - gain_sin * part_re)
        ):
            folded = value[:, :128]
            for lane in range(128, width, 128):
                folded = folded + value[:, lane : lane + 128]
            out_ref[0, part : part + 1, rows] = jnp.sum(folded.T, axis=0, keepdims=True)


def per_device(image, deapodization, offsets, cross_weight, x_weight):
    wide_count = lax.axis_size("wide")
    narrow_count = lax.axis_size("narrow")
    wide_index = lax.axis_index("wide")
    narrow_index = lax.axis_index("narrow")
    block_x = image.shape[1]
    block_y = image.shape[2]
    width = image.shape[3]
    depth = KZ // narrow_count
    samples, cells = cross_weight.shape[2], cross_weight.shape[3]
    scale_x = lax.dynamic_slice_in_dim(deapodization[0], wide_index * block_x, block_x)
    scale_y = lax.dynamic_slice_in_dim(deapodization[1], narrow_index * block_y, block_y)
    weighted = (
        image.astype(jnp.float32)
        * scale_x[None, :, None, None]
        * scale_y[None, None, :, None]
        * deapodization[2][None, None, None, :]
    ).astype(jnp.bfloat16)
    z_table = complex_table(*base_tables(KZ, width, G, -(KZ // 2)))
    band = jnp.einsum(
        "okcz,cxyz->kxoy", jnp.asarray(z_table), weighted, preferred_element_type=jnp.float32
    ).astype(jnp.bfloat16)
    band = band.reshape(KZ, block_x, 2 * block_y)
    band = lax.all_to_all(band, "narrow", split_axis=0, concat_axis=0, tiled=True)
    band = lax.all_gather(band, "wide", axis=0, tiled=False)
    band = band.reshape(wide_count, narrow_count, depth, block_x, 2 * block_y)
    if (2 * block_y) % 128:
        band = band.transpose(0, 2, 3, 1, 4).reshape(wide_count, 1, depth, block_x, 2 * width)

    cosine, sine = base_tables(G, width, G, -(G // 2))
    line_table = complex_table(cosine, sine).reshape(2 * G, 2, narrow_count, block_y)
    line_table = line_table.transpose(0, 2, 1, 3).reshape(2 * G, 2 * width)
    row_table = np.concatenate([cosine, sine], axis=1).astype(np.float32)
    row_table = row_table.reshape(G, 2 * width // 128, 128).transpose(1, 0, 2)

    tile = 512 if samples % 512 == 0 else samples
    kernel = functools.partial(sample_kernel, (depth, G, width, tile))
    out = pl.pallas_call(
        kernel,
        grid=(wide_count,),
        out_shape=jax.ShapeDtypeStruct((wide_count, 2, samples), jnp.float32),
        in_specs=[
            pl.BlockSpec(memory_space=pltpu.SMEM),
            pl.BlockSpec(band.shape, lambda s: (0, 0, 0, 0, 0)),
            pl.BlockSpec(line_table.shape, lambda s: (0, 0)),
            pl.BlockSpec(row_table.shape, lambda s: (0, 0, 0)),
            pl.BlockSpec((1, samples, BX), lambda s: (s, 0, 0)),
            pl.BlockSpec((1, samples, cells), lambda s: (s, 0, 0)),
        ],
        out_specs=pl.BlockSpec((1, 2, samples), lambda s: (s, 0, 0)),
        scratch_shapes=[
            pltpu.VMEM((2 * width // 128, G * depth, 128), jnp.float32),
            pltpu.VMEM((cells, 2 * width), jnp.bfloat16),
            pltpu.VMEM((BX, 2 * width), jnp.bfloat16),
        ],
        compiler_params=pltpu.CompilerParams(vmem_limit_bytes=60 * 1024 * 1024),
        cost_estimate=pl.CostEstimate(
            flops=2 * wide_count * samples * 2 * width * (cells + BX) + 8 * G * width * width * depth,
            bytes_accessed=2 * wide_count * samples * (cells + BX),
            transcendentals=0,
        ),
    )(offsets, band, jnp.asarray(line_table), jnp.asarray(row_table), x_weight[0], cross_weight[0])
    return out[None]


def solution(mesh):
    return jax.shard_map(
        per_device,
        mesh=mesh,
        in_specs=(
            P(None, "wide", "narrow", None),
            P(),
            P(("wide", "narrow"), None),
            P(("wide", "narrow"), None, None, None),
            P(("wide", "narrow"), None, None, None),
        ),
        out_specs=P(("wide", "narrow"), None, None, None),
        check_vma=False,
    )
```

time: 223 us -> 107 us (0.48)
  local copies, waits for them, and re-layouts: 73.5 us -> 1.78 us
  matrix products: 41.5 us -> 2.53 us
  other arithmetic: 37.8 us -> 0 us
  Pallas kernels: 0 us -> 32.7 us
  waiting for transfers between devices: 58.2 us -> 35.9 us
  blocking collectives: 0 us -> 20.7 us
  between operations: 0.16 us -> 13.4 us
  starting transfers between devices: 10.1 us -> 0.01 us
    dot_general x10 -> x1, matrix products: 41.5 us -> 2.53 us  [per_device(): jnp.einsum('okcz,cxyz->kxoy', jnp.asarray(z_table), weighted, preferred_e...]
    ppermute x7 -> x0, waiting for transfers between devices: 38.5 us -> none  [shifted(): return lax.ppermute(block, axis, route)]
    all_gather x0 -> x1, waiting for transfers between devices: none -> 35.8 us  [per_device(): band = lax.all_gather(band, 'wide', axis=0, tiled=False)]
    pallas_call x0 -> x1, Pallas kernels: none -> 32.7 us  [per_device(): pl.pallas_call(kernel, grid=(wide_count,), out_shape=jax.ShapeDtypeStruct...]
    all_to_all x0 -> x1, blocking collectives: none -> 20.7 us  [per_device(): lax.all_to_all(band, 'narrow', split_axis=0, concat_axis=0, tiled=True)]
    all_to_all x2 -> x0, waiting for transfers between devices: 19.7 us -> none  [the longest x1 10 us: per_device(): lax.all_to_all(columns, 'wide', split_axis=2, concat_axis=0, tiled=True)]
    another operation x7 -> x0, local copies, waits for them, and re-layouts: 15.8 us -> none
    convert_element_type x18 -> x0, other arithmetic: 15.6 us -> none  [the longest x10 13.1 us: block_table(): sine = (jnp.sin(angles) * factor).astype(jnp.bfloat16)]
  transfers between devices with their start and end apart: 9 -> 1, of which waited for: 9 -> 1; matrix products, arithmetic and copies ran while one was open for 36% -> 0% of each run, Pallas kernels for 0% -> 0%
where the time goes in v1:
time: 107 us
  waiting for transfers between devices  35.9 us (34%)
  Pallas kernels  32.7 us (31%)
  blocking collectives  20.7 us (19%)
  between operations  13.4 us (13%)
  matrix products  2.53 us (2%)
  local copies, waits for them, and re-layouts  1.78 us (2%)
    all_gather x1, waiting for transfers between devices, per_device(): band = lax.all_gather(band, 'wide', axis=0, tiled=False)  35.8 us
    pallas_call x1, Pallas kernels, per_device(): pl.pallas_call(kernel, grid=(wide_count,), out_shape=jax.ShapeDtypeStruct...  32.7 us
    all_to_all x1, blocking collectives, per_device(): lax.all_to_all(band, 'narrow', split_axis=0, concat_axis=0, tiled=True)  20.7 us
    dot_general x1, matrix products, per_device(): jnp.einsum('okcz,cxyz->kxoy', jnp.asarray(z_table), weighted, preferred_e...  2.53 us
  transfers between devices with their start and end apart: 1, of which 1 were waited for; matrix products, arithmetic and copies ran while one was open for 0% of the time, Pallas kernels for 0%

profile of v1, /device:TPU:0, one launch (start us, length us, event | category | flops | bytes accessed | tf_op | source)
XLA Modules:
  0.0 107.0 jit_solution(12865037245932334744)
XLA Ops:
  6.5 0.0 all-gather.3.cloned.1.call-start
  6.5 0.8 fusion.5
  7.3 0.1 dynamic-slice_bitcast_fusion
  7.4 0.1 dynamic-slice_bitcast_fusion.1
  7.5 2.5 %bitcast_convert_fusion = bf16[32,64,2,64]{3,1,2,0:T(8,128)(2,1)S(1)} fusion(bf16[2,64,2,256,1]{3,1,2,0,4:T(8,128)(2,1)} %constant.31, bf16[2,32,64,256]{3,2,1,0:T(8,128)(2,1)} %param.8, f32[256]{0:T(256)S(1)} %bitcast.22, f32[64]{0:T(128)S(1)} %dynamic-slice_bitcast_fusion, f32[32]{0:T(128)S(1)} %dynamic-slice_bitcast_fusion.1), kind=kOutput, calls=%fused_computation.2 | convolution fusion | flops 273940480 | bytes 2753920 | tf_op jit(solution)/shard_map/okcz,cxyz->kxoy/dot_general | solution.py:102
  10.0 0.8 copy.12
  10.9 20.7 %all_to_all.5 = bf16[64,32,128]{2,1,0:T(8,128)(2,1)} all-to-all(bf16[64,32,128]{2,1,0:T(8,128)(2,1)S(1)} %copy.12), channel_id=1, replica_groups=mesh['wide'=8,'narrow'=4] {'narrow'}, dimensions={0} | all-to-all | bytes 1048576 | tf_op jit(solution)/shard_map/all_to_all | solution.py:106
  31.6 0.0 all-gather.3.cloned.1.call-update
  31.6 35.8 %all-gather.3.cloned.1.call-done = bf16[512,32,128]{2,1,0:T(8,128)(2,1)} async-done(((bf16[64,32,128]{2,1,0:T(8,128)(2,1)}), bf16[512,32,128]{2,1,0:T(8,128)(2,1)}) %all-gather.3.cloned.1.call-update) | async-done | bytes 4194320 | tf_op jit(solution)/shard_map/all_gather | solution.py:107
  67.5 32.7 %shard_map.82 = f32[8,2,1536]{2,1,0:T(2,128)} custom-call(s32[1,8]{1,0:T(1,128)} %offsets_ref.1, bf16[8,4,16,32,128]{4,3,2,1,0:T(8,128)(2,1)} %bitcast.25, bf16[1024,512]{1,0:T(8,128)(2,1)} %constant.26.clone.line_ref, f32[4,512,128]{2,1,0:T(8,128)} %constant.27.clone.row_ref, bf16[8,1536,256]{2,1,0:T(8,128)(2,1)} %bitcast.24, bf16[8,1536,1024]{2,1,0:T(8,128)(2,1)} %bitcast.23), custom_call_target="tpu_custom_call" | custom-call | flops 20401094656 | bytes 31457280 | tf_op jit(solution)/shard_map/pallas_call | solution.py:120
Async XLA Ops:
  6.5 60.9 %all-gather.3.cloned.1.call-start = ((), (), s32[]{:S(2)}) async-start(), calls=%async_computation.1 | async-start | bytes 4718592 | tf_op jit(solution)/shard_map/all_gather | solution.py:107
Sparse Core Ops, SparseCore 0:
  31.7 35.6 all-gather.2

commit v2 on v1

--- a/solution.py
+++ b/solution.py
@@ -78,6 +78,66 @@
             for lane in range(128, width, 128):
                 folded = folded + value[:, lane : lane + 128]
             out_ref[0, part : part + 1, rows] = jnp.sum(folded.T, axis=0, keepdims=True)
+
+
+def gather_kernel(
+    wide, narrow, band_ref, out_ref, own_sem, swap_send, swap_recv, chip_send, chip_recv, core_send, core_recv
+):
+    w = lax.axis_index("wide")
+    n = lax.axis_index("narrow")
+    sibling = w + 1 - 2 * lax.rem(w, 2)
+    chips = wide // 2
+    barrier = pltpu.get_barrier_semaphore()
+    targets = [(w, lax.rem(n + j, narrow)) for j in range(1, narrow)]
+    targets += [(lax.rem(w + 2 * j, wide), n) for j in range(1, chips)] + [(sibling, n)]
+    for target in targets:
+        pl.semaphore_signal(
+            barrier, inc=1, device_id=target, device_id_type=pl.DeviceIdType.MESH
+        )
+    pl.semaphore_wait(barrier, len(targets))
+
+    def remote(source, place, send, receive, target):
+        return pltpu.make_async_remote_copy(
+            src_ref=source,
+            dst_ref=place,
+            send_sem=send,
+            recv_sem=receive,
+            device_id=target,
+            device_id_type=pl.DeviceIdType.MESH,
+        )
+
+    swaps = []
+    for j in range(1, narrow):
+        peer = lax.rem(n + j, narrow)
+        swap = remote(
+            band_ref.at[peer], out_ref.at[w, n], swap_send.at[j - 1], swap_recv.at[j - 1], (w, peer)
+        )
+        swap.start()
+        swaps.append(swap)
+    own = pltpu.make_async_copy(band_ref.at[n], out_ref.at[w, n], own_sem)
+    own.start()
+    own.wait()
+    for swap in swaps:
+        swap.wait()
+    mine = out_ref.at[w]
+    hops = []
+    for j in range(1, chips):
+        peer = lax.rem(w + 2 * j, wide)
+        hop = remote(mine, mine, chip_send.at[j - 1], chip_recv.at[j - 1], (peer, n))
+        hop.start()
+        hops.append(hop)
+    passes = [remote(mine, mine, core_send.at[0], core_recv.at[0], (sibling, n))]
+    passes[0].start()
+    for j in range(1, chips):
+        hops[j - 1].wait_recv()
+        block = out_ref.at[lax.rem(w + wide - 2 * j, wide)]
+        forward = remote(block, block, core_send.at[j], core_recv.at[j], (sibling, n))
+        forward.start()
+        passes.append(forward)
+    for hop in hops:
+        hop.wait_send()
+    for forward in passes:
+        forward.wait()
 
 
 def per_device(image, deapodization, offsets, cross_weight, x_weight):
@@ -103,9 +163,24 @@
         "okcz,cxyz->kxoy", jnp.asarray(z_table), weighted, preferred_element_type=jnp.float32
     ).astype(jnp.bfloat16)
     band = band.reshape(KZ, block_x, 2 * block_y)
-    band = lax.all_to_all(band, "narrow", split_axis=0, concat_axis=0, tiled=True)
-    band = lax.all_gather(band, "wide", axis=0, tiled=False)
-    band = band.reshape(wide_count, narrow_count, depth, block_x, 2 * block_y)
+    band = band.reshape(narrow_count, depth, block_x, 2 * block_y)
+    chips = wide_count // 2
+    band = pl.pallas_call(
+        functools.partial(gather_kernel, wide_count, narrow_count),
+        out_shape=jax.ShapeDtypeStruct((wide_count,) + band.shape, band.dtype),
+        in_specs=[pl.BlockSpec(memory_space=pltpu.VMEM)],
+        out_specs=pl.BlockSpec(memory_space=pltpu.VMEM),
+        scratch_shapes=[
+            pltpu.SemaphoreType.DMA,
+            pltpu.SemaphoreType.DMA((narrow_count - 1,)),
+            pltpu.SemaphoreType.DMA((narrow_count - 1,)),
+            pltpu.SemaphoreType.DMA((chips - 1,)),
+            pltpu.SemaphoreType.DMA((chips - 1,)),
+            pltpu.SemaphoreType.DMA((chips,)),
+            pltpu.SemaphoreType.DMA((chips,)),
+        ],
+        compiler_params=pltpu.CompilerParams(collective_id=0, has_side_effects=True),
+    )(band)
     if (2 * block_y) % 128:
         band = band.transpose(0, 2, 3, 1, 4).reshape(wide_count, 1, depth, block_x, 2 * width)
 

time: 107 us -> 84.1 us (0.79)
  the two profiles are of different devices: /device:TPU:0 before, /device:TPU:11 now
where the time goes in v2:
time: 84.1 us; the launch traced here: 83.9 us
  Pallas kernels  78 us (93%)
  local copies, waits for them, and re-layouts  3.3 us (4%)
  matrix products  2.53 us (3%)
    pallas_call x1, Pallas kernels, per_device(): pl.pallas_call(functools.partial(gather_kernel, wide_count, narrow_count)...  45.3 us
    pallas_call x1, Pallas kernels, per_device(): pl.pallas_call(kernel, grid=(wide_count,), out_shape=jax.ShapeDtypeStruct...  32.7 us
    dot_general x1, matrix products, per_device(): jnp.einsum('okcz,cxyz->kxoy', jnp.asarray(z_table), weighted, preferred_e...  2.53 us

profile of v2, /device:TPU:11, one launch (start us, length us, event | category | flops | bytes accessed | tf_op | source)
XLA Modules:
  0.0 83.9 jit_solution(10297580652680264839)
XLA Ops:
  0.0 0.8 fusion.8
  0.8 0.1 dynamic-slice_bitcast_fusion
  0.9 0.1 dynamic-slice_bitcast_fusion.1
  0.9 2.5 %fusion.5 = bf16[64,32,2,64]{0,3,2,1:T(8,128)(2,1)S(1)} fusion(bf16[2,64,2,256,1]{3,1,2,0,4:T(8,128)(2,1)} %constant.31, bf16[2,32,64,256]{3,2,1,0:T(8,128)(2,1)} %param.8, f32[256]{0:T(256)S(1)} %bitcast.21, f32[64]{0:T(128)S(1)} %dynamic-slice_bitcast_fusion, f32[32]{0:T(128)S(1)} %dynamic-slice_bitcast_fusion.1), kind=kOutput, calls=%fused_computation.5 | convolution fusion | flops 273940480 | bytes 2753920 | tf_op jit(solution)/shard_map/okcz,cxyz->kxoy/dot_general | solution.py:162
  3.5 1.1 %copy.10 = bf16[64,32,2,64]{3,2,1,0:T(2,128)(2,1)S(1)} copy(bf16[64,32,2,64]{0,3,2,1:T(8,128)(2,1)S(1)} %fusion.5) | data formatting | bytes 1048576 | tf_op jit(solution)/shard_map/convert_element_type | solution.py:164
  4.6 1.3 %reshape_reshape.3.band_ref = bf16[4,16,32,128]{3,2,1,0:T(8,128)(2,1)} reshape(bf16[64,32,2,64]{3,2,1,0:T(2,128)(2,1)S(1)} %copy.10) | data formatting | bytes 1048576 | tf_op jit(solution)/shard_map/reshape;reshape | solution.py:166
  5.8 45.3 %shard_map.82.band_ref = bf16[8,4,16,32,128]{4,3,2,1,0:T(8,128)(2,1)} custom-call(bf16[4,16,32,128]{3,2,1,0:T(8,128)(2,1)} %reshape_reshape.3.band_ref), custom_call_target="tpu_custom_call" | custom-call | tf_op jit(solution)/shard_map/pallas_call | solution.py:168
  51.1 32.7 %shard_map.83 = f32[8,2,1536]{2,1,0:T(2,128)} custom-call(s32[1,8]{1,0:T(1,128)} %offsets_ref.1, bf16[8,4,16,32,128]{4,3,2,1,0:T(8,128)(2,1)} %shard_map.82.band_ref, bf16[1024,512]{1,0:T(8,128)(2,1)} %constant.26.clone.line_ref, f32[4,512,128]{2,1,0:T(8,128)} %constant.27.clone.row_ref, bf16[8,1536,256]{2,1,0:T(8,128)(2,1)} %bitcast.23, ...), custom_call_target="tpu_custom_call" | custom-call | flops 20401094656 | bytes 31457280 | tf_op jit(solution)/shard_map/pallas_call | solution.py:195
